TPU v7x, 32 devices: a whole 2x2x4 slice. The times are simulated.
32 devices in a mesh: dp: 2 (over x), tp: 4 (over z), sp: 4 (over y, core).
Axes of the slice: x: 2, y: 2, z: 4, core: 2. Of those that a mesh axis runs over, the one named last changes fastest.
Arguments:
- tok_hidden: bfloat16 [512, 4096], P('dp'), parts along dimension 0
- cache_len: int32 [512], P('dp'), parts along dimension 0
- k_cache: bfloat16 [512, 32, 64, 128], P('dp', 'tp', 'sp'), parts along dimension 0
- v_cache: bfloat16 [512, 32, 64, 128], P('dp', 'tp', 'sp'), parts along dimension 0
- ln_gain: float32 [4096], replicated
- ln_bias: float32 [4096], replicated
- w_qkv: bfloat16 [4096, 3, 32, 128], P(None, None, 'tp')
- b_qkv: bfloat16 [3, 32, 128], P(None, 'tp')
- w_out: bfloat16 [32, 128, 4096], P('tp')
- b_out: bfloat16 [4096], replicated
Outputs:
- output 1: bfloat16 [512, 4096], P('dp'), parts along dimension 0
- output 2: bfloat16 [512, 32, 64, 128], P('dp', 'tp', 'sp'), parts along dimension 0
- output 3: bfloat16 [512, 32, 64, 128], P('dp', 'tp', 'sp'), parts along dimension 0
There are 2 independent parts. A program takes and returns all parts, laid end to end along the dimension named above; an argument that names none is the same for every part.
All inputs are finite; a program needn't handle non-finite values.
Results may differ from a plain program's by a relative error of at most 0.00849222.
Values sent between devices are 32-bit elements.
A program may use at most 1 GiB of HBM per device.

v0:
```python
import jax
import jax.numpy as jnp
from jax import lax
from jax.sharding import PartitionSpec as P, NamedSharding


def norm_project(tok_hidden, ln_gain, ln_bias, w_qkv, b_qkv):
    x_f32 = tok_hidden.astype(jnp.float32)
    mean_x = jnp.mean(x_f32, axis=-1, keepdims=True)
    centered = x_f32 - mean_x
    var_x = jnp.mean(centered * centered, axis=-1, keepdims=True)
    hidden = (centered * lax.rsqrt(var_x + 1e-5) * ln_gain + ln_bias).astype(jnp.bfloat16)
    qkv_all = jnp.einsum('bm,mthd->bthd', hidden, w_qkv, preferred_element_type=jnp.float32)
    qkv_all = (qkv_all + b_qkv.astype(jnp.float32)).astype(jnp.bfloat16)
    return x_f32, qkv_all[:, 0], qkv_all[:, 1], qkv_all[:, 2]


def write_token(cache, new_row, local_len):
    slots = jnp.arange(cache.shape[2], dtype=jnp.int32)
    write_mask = (slots[None, :] == local_len[:, None])[:, None, :, None]
    return jnp.where(write_mask, new_row[:, :, None, :], cache)


def solution(mesh):
    cache_spec = P('dp', 'tp', 'sp', None)
    row_spec = P('dp', None)

    def local_block(tok_hidden, cache_len, k_cache, v_cache, ln_gain, ln_bias, w_qkv, b_qkv, w_out, b_out):
        head_dim = k_cache.shape[3]
        seq_local = k_cache.shape[2]
        x_f32, q_new, k_new, v_new = norm_project(tok_hidden, ln_gain, ln_bias, w_qkv, b_qkv)
        local_len = cache_len - lax.axis_index('sp') * seq_local
        k_out = write_token(k_cache, k_new, local_len)
        v_out = write_token(v_cache, v_new, local_len)
        slots = jnp.arange(seq_local, dtype=jnp.int32)
        scores = jnp.einsum('bhd,bhsd->bhs', q_new, k_out, preferred_element_type=jnp.float32) * head_dim ** -0.5
        valid = (slots[None, :] <= local_len[:, None])[:, None, :]
        masked = jnp.where(valid, scores, -1e30)
        local_max = jnp.max(masked, axis=-1)
        weights = jnp.where(valid, jnp.exp(masked - local_max[..., None]), 0.0)
        local_sum = jnp.sum(weights, axis=-1)
        local_acc = jnp.einsum('bhs,bhsd->bhd', weights.astype(jnp.bfloat16), v_out, preferred_element_type=jnp.float32)
        global_max = lax.pmax(local_max, 'sp')
        factor = jnp.exp(local_max - global_max)
        combined_in = jnp.concatenate([local_acc * factor[..., None], (local_sum * factor)[..., None]], axis=-1)
        totals = lax.psum(combined_in, 'sp')
        attended = (totals[..., :head_dim] / totals[..., head_dim:]).astype(jnp.bfloat16)
        partial_out = jnp.einsum('bhd,hdm->bm', attended, w_out, preferred_element_type=jnp.float32)
        projected = lax.psum(partial_out, 'tp')
        y_out = (x_f32 + projected + b_out.astype(jnp.float32)).astype(jnp.bfloat16)
        return y_out, k_out, v_out

    return jax.shard_map(
        local_block,
        mesh=mesh,
        in_specs=(row_spec, P('dp'), cache_spec, cache_spec, P(None), P(None), P(None, None, 'tp', None), P(None, 'tp', None), P('tp', None, None), P(None)),
        out_specs=(row_spec, cache_spec, cache_spec),
        check_vma=False,
    )
```

profile of v0, /device:TPU:1, one launch (start us, length us, event | category | flops | bytes accessed | tf_op | source)
XLA Modules:
  0.0 285.1 jit_solution(5494819765346046107)
XLA Ops:
  7.2 0.0 copy-start
  7.2 0.0 copy-start.4
  7.2 0.0 copy-start.7
  7.2 0.0 copy-start.6
  7.2 0.0 all-reduce.3.cloned.1.call-start
  7.3 2.1 convert_reduce_fusion
  9.3 2.3 fusion.9
  11.6 0.0 copy-done.4
  11.7 0.0 copy-done
  11.7 0.0 copy-done.7
  11.7 0.0 copy-done.6
  11.7 16.1 %add_convert_fusion = bf16[256,3,8,128]{3,0,2,1:T(8,128)(2,1)} fusion(bf16[4096,3,8,128]{3,2,1,0:T(8,128)(2,1)} %param.16, bf16[256,4096]{1,0:T(8,128)(2,1)S(1)} %copy-done, f32[4096]{0:T(1024)S(1)} %copy-done.6, f32[4096]{0:T(1024)S(1)} %copy-done.7, f32[256]{0:T(256)S(1)} %add_rsqrt_fusion, f32[256]{0:T(256)S(1)} %broadcast_multiply_fusion.1, ...), kind=kOutput, calls=%fused_computation.19 | convolution fusion | flops 6450315264 | bytes 28882944 | tf_op jit(solution)/shard_map/bm,mthd->bthd/dot_general | solution.py:13
  27.8 0.0 copy-start.5
  27.8 2.5 slice_bitcast_fusion
  30.2 0.3 copy.24
  30.6 0.0 copy-done.5
  30.6 0.1 iota_compare_fusion.1
  30.7 0.0 copy-start.2
  30.7 4.6 %broadcast_select_fusion.1 = bf16[256,8,16,128]{3,2,1,0:T(8,128)(2,1)S(1)} fusion(bf16[256,8,16,128]{3,2,1,0:T(8,128)(2,1)} %param.12, pred[256,16]{1,0:T(8,128)(4,1)S(1)} %get-tuple-element.13, bf16[256,8,128]{2,1,0:T(8,128)(2,1)S(1)} %copy.24), kind=kLoop, calls=%fused_computation.6 | loop fusion | flops 4194304 | bytes 17305600 | tf_op jit(solution)/shard_map/jit(_where)/select_n | solution.py:21
  35.4 0.0 copy-start.1
  35.4 3.4 %copy-done.1 = bf16[256,8,16,128]{3,2,1,0:T(8,128)(2,1)} copy-done((bf16[256,8,16,128]{3,2,1,0:T(8,128)(2,1)}, bf16[256,8,16,128]{3,2,1,0:T(8,128)(2,1)S(1)}, u32[]{:S(2)}) %copy-start.1) | copy-done | bytes 8388632
  38.8 0.0 copy-done.2
  38.8 4.6 %fusion.26 = f32[256,8,1,16]{3,2,1,0:T(1,128)S(1)} fusion(bf16[256,8,16,128]{3,2,1,0:T(8,128)(2,1)S(1)} %broadcast_select_fusion.1, bf16[256,8,128,1]{2,0,1,3:T(8,128)(2,1)S(1)} %copy-done.2), kind=kOutput, calls=%fused_computation.28 | convolution fusion | flops 8388608 | bytes 9043968 | tf_op jit(solution)/shard_map/bhd,bhsd->bhs/dot_general | solution.py:36
  43.4 0.8 copy.29
  44.2 0.1 copy.22
  44.3 0.1 fusion.34
  44.4 6.7 %pmax.7 = f32[256,8]{0,1:T(8,128)S(1)} all-reduce(f32[256,8]{0,1:T(8,128)S(1)} %fusion.31), channel_id=1, replica_groups=mesh['dp'=2,'tp'=4,'sp'=4] {'sp'}, use_global_device_ids=true, to_apply=%region_3.4 | all-reduce | flops 2048 | bytes 16384 | tf_op jit(solution)/shard_map/pmax | solution.py:43
  51.0 0.4 copy.35
  51.4 1.4 copy.25
  52.8 14.1 %multiply_reduce_fusion = (f32[256,8,128]{2,1,0:T(8,128)}, bf16[256,8,16,128]{3,2,1,0:T(8,128)(2,1)}) fusion(f32[256,8,16]{2,1,0:T(8,128)S(1)} %copy.35, bf16[256,8,16,128]{3,2,1,0:T(8,128)(2,1)} %param.13, bf16[256,8,128]{2,1,0:T(8,128)(2,1)S(1)} %copy.25, pred[256,16]{1,0:T(8,128)(4,1)S(1)} %get-tuple-element.13), kind=kLoop, calls=%fused_computation.2 | loop fusion | flops 16515072 | bytes 18485248
  66.9 1.7 copy.34
  68.7 0.1 broadcast_multiply_fusion
  68.8 1.0 pad_maximum_fusion
  69.8 0.0 all-reduce.3.cloned.1.call-update
  69.8 0.0 all-reduce.5.cloned.1.call-start
  69.9 38.0 %all-reduce.3.cloned.1.call-done = f32[256,8,129]{0,1,2:T(8,128)} async-done(((f32[256,8,129]{0,1,2:T(8,128)}), f32[256,8,129]{0,1,2:T(8,128)}) %all-reduce.3.cloned.1.call-update) | async-done | bytes 1056784 | tf_op jit(solution)/shard_map/psum | solution.py:46
  107.9 0.7 slice_bitcast_fusion.3
  108.6 11.2 %fusion.4 = f32[256,4096]{1,0:T(8,128)} fusion(bf16[8,128,4096]{2,1,0:T(8,128)(2,1)} %param.18, f32[256,8,129]{0,1,2:T(8,128)} %all-reduce.3.cloned.1.call-done, f32[256,8]{0,1:T(8,128)S(1)} %slice_bitcast_fusion.3), kind=kOutput, calls=%fused_computation.10 | convolution fusion | flops 2148007936 | bytes 13639680 | tf_op jit(solution)/shard_map/bhd,hdm->bm/dot_general | solution.py:48
  119.8 0.0 copy-start.3
  119.8 0.0 all-reduce.5.cloned.1.call-update
  119.8 0.7 copy-done.3
  120.5 153.7 %all-reduce.5.cloned.1.call-done = f32[256,4096]{1,0:T(8,128)} async-done(((f32[256,4096]{1,0:T(8,128)}), f32[256,4096]{1,0:T(8,128)}) %all-reduce.5.cloned.1.call-update) | async-done | bytes 4194320 | tf_op jit(solution)/shard_map/psum | solution.py:49
  274.2 4.1 %fusion.14 = bf16[256,4096]{1,0:T(8,128)(2,1)} fusion(f32[256,4096]{1,0:T(8,128)} %all-reduce.5.cloned.1.call-done, bf16[256,4096]{1,0:T(8,128)(2,1)S(1)} %copy-done, f32[4096]{0:T(1024)S(1)} %convert_element_type.30), kind=kLoop, calls=%fused_computation.18 | loop fusion | flops 4194304 | bytes 8404992 | tf_op jit(solution)/shard_map/convert_element_type | solution.py:50
  (7 shorter events, 0.1 us)
Async XLA Ops:
  7.2 4.5 %copy-start = (bf16[256,4096]{1,0:T(8,128)(2,1)S(1)}, bf16[256,4096]{1,0:T(8,128)(2,1)}, u32[]{:S(2)}) copy-start(bf16[256,4096]{1,0:T(8,128)(2,1)} %param.10) | copy-start | bytes 6291460
  7.2 4.5 %copy-start.4 = (bf16[3,8,128]{2,1,0:T(8,128)(2,1)S(1)}, bf16[3,8,128]{2,1,0:T(8,128)(2,1)}, u32[]{:S(2)}) copy-start(bf16[3,8,128]{2,1,0:T(8,128)(2,1)} %param.17) | copy-start | bytes 18436
  7.2 4.5 %copy-start.7 = (f32[4096]{0:T(1024)S(1)}, f32[4096]{0:T(1024)}, u32[]{:S(2)}) copy-start(f32[4096]{0:T(1024)} %param.14) | copy-start | bytes 49156
  7.2 4.5 %copy-start.6 = (f32[4096]{0:T(1024)S(1)}, f32[4096]{0:T(1024)}, u32[]{:S(2)}) copy-start(f32[4096]{0:T(1024)} %param.15) | copy-start | bytes 49156
  7.2 100.7 %all-reduce.3.cloned.1.call-start = ((), (), s32[]{:S(2)}) async-start(), calls=%async_computation | async-start | bytes 2113536 | tf_op jit(solution)/shard_map/psum | solution.py:46
  27.8 2.8 copy-start.5
  30.7 8.1 %copy-start.2 = (bf16[256,8,128,1]{2,0,1,3:T(8,128)(2,1)S(1)}, bf16[256,8,128,1]{2,0,1,3:T(8,128)(2,1)}, u32[]{:S(2)}) copy-start(bf16[256,8,128,1]{2,0,1,3:T(8,128)(2,1)} %get-tuple-element.9) | copy-start | bytes 1572868
  35.4 3.4 %copy-start.1 = (bf16[256,8,16,128]{3,2,1,0:T(8,128)(2,1)}, bf16[256,8,16,128]{3,2,1,0:T(8,128)(2,1)S(1)}, u32[]{:S(2)}) copy-start(bf16[256,8,16,128]{3,2,1,0:T(8,128)(2,1)S(1)} %broadcast_select_fusion.1) | copy-start | bytes 25165828
  69.8 204.3 %all-reduce.5.cloned.1.call-start = ((), (), s32[]{:S(2)}) async-start(), calls=%async_computation.1 | async-start | bytes 8388608 | tf_op jit(solution)/shard_map/psum | solution.py:49
  119.8 0.7 copy-start.3
Sparse Core Ops, SparseCore 0:
  70.0 37.8 all-reduce.2
  119.9 154.1 all-reduce.4
where the time goes:
time: 287 us; the launch traced here: 285 us
  waiting for transfers between devices  192 us (67%)
  matrix products  31.8 us (11%)
  other arithmetic  28.6 us (10%)
  between operations  14.2 us (5%)
  local copies, waits for them, and re-layouts  12 us (4%)
  blocking collectives  6.66 us (2%)
    psum x1, waiting for transfers between devices, local_block(): projected = lax.psum(partial_out, 'tp')  154 us
    psum x1, waiting for transfers between devices, local_block(): totals = lax.psum(combined_in, 'sp')  38 us
    dot_general x1, matrix products, norm_project(): jnp.einsum('bm,mthd->bthd', hidden, w_qkv, preferred_element_type=jnp.flo...  16.1 us
    unnamed x2, other arithmetic  14.2 us
    dot_general x1, matrix products, local_block(): jnp.einsum('bhd,hdm->bm', attended, w_out, preferred_element_type=jnp.flo...  11.2 us
    pmax x1, blocking collectives, local_block(): global_max = lax.pmax(local_max, 'sp')  6.66 us
  transfers between devices with their start and end apart: 2, of which 2 were waited for; matrix products, arithmetic and copies ran while one was open for 0% of the time, Pallas kernels for 0%

commit v1 on v0

v1 whole, which is shorter than its diff:
```python
import functools

import jax
import jax.numpy as jnp
from jax import lax
from jax.experimental import pallas as pl
from jax.experimental.pallas import tpu as pltpu
from jax.sharding import PartitionSpec as P

MESH = pl.DeviceIdType.MESH
NEG = -1e30
F32 = jnp.float32
BF16 = jnp.bfloat16


def norm_project(tok_hidden, ln_gain, ln_bias, w_qkv, b_qkv):
    x_f32 = tok_hidden.astype(F32)
    mean_x = jnp.mean(x_f32, axis=-1, keepdims=True)
    centered = x_f32 - mean_x
    var_x = jnp.mean(centered * centered, axis=-1, keepdims=True)
    hidden = (centered * lax.rsqrt(var_x + 1e-5) * ln_gain + ln_bias).astype(BF16)
    qkv_all = jnp.einsum('bm,mthd->thbd', hidden, w_qkv, preferred_element_type=F32)
    return (qkv_all + b_qkv.astype(F32)[:, :, None, :]).astype(BF16)


def attend_kernel(slots, per_stat, len_ref, qkv_ref, k_ref, v_ref, ko_ref, vo_ref, acc_ref, st_ref, qkv_f32):
    rows, heads, _, dim = k_ref.shape
    step = pl.program_id(0)
    first = lax.axis_index('sp') * slots
    qkv_f32[...] = qkv_ref[...].astype(F32)
    slot = lax.broadcasted_iota(jnp.int32, (slots, dim), 0)
    flat = heads * slots
    row_id = lax.broadcasted_iota(jnp.int32, (heads, flat), 0)
    col_id = lax.broadcasted_iota(jnp.int32, (heads, flat), 1)
    in_head = (col_id // slots) == row_id
    col_slot = jnp.where(in_head, col_id % slots, slots)
    lane = lax.broadcasted_iota(jnp.int32, (heads, 128), 1)
    group = lax.rem(step, per_stat // rows)

    @pl.when(group == 0)
    def _():
        st_ref[...] = jnp.zeros_like(st_ref)

    stat = st_ref[0]
    for b in range(rows):
        local = len_ref[step * rows + b] - first
        hit = (slot == local)[None]
        k_new = jnp.broadcast_to(qkv_f32[1, :, b:b + 1, :], (heads, slots, dim)).astype(BF16)
        v_new = jnp.broadcast_to(qkv_f32[2, :, b:b + 1, :], (heads, slots, dim)).astype(BF16)
        k_all = jnp.where(hit, k_new, k_ref[b])
        v_all = jnp.where(hit, v_new, v_ref[b])
        ko_ref[b] = k_all
        vo_ref[b] = v_all
        q = qkv_f32[0, :, b, :].astype(BF16)
        s = lax.dot_general(q, k_all.reshape(flat, dim), (((1,), (1,)), ((), ())), preferred_element_type=F32)
        valid = col_slot <= jnp.minimum(local, slots - 1)
        s = jnp.where(valid, s * dim ** -0.5, NEG)
        top = jnp.max(s, axis=1, keepdims=True)
        w = jnp.where(valid, jnp.exp(s - top), 0.0)
        total = jnp.sum(w, axis=1, keepdims=True)
        acc_ref[b] = jnp.dot(w.astype(BF16), v_all.reshape(flat, dim), preferred_element_type=F32)
        at = group * rows + b
        stat = jnp.where(lane == at, top, stat)
        stat = jnp.where(lane == per_stat + at, total, stat)
    st_ref[0] = stat


def attend(qkv, cache_len, k_cache, v_cache, block, per_stat):
    rows, heads, slots, dim = k_cache.shape
    cache_block = pl.BlockSpec((block, heads, slots, dim), lambda i: (i, 0, 0, 0))
    return pl.pallas_call(
        functools.partial(attend_kernel, slots, per_stat),
        grid=(rows // block,),
        in_specs=[
            pl.BlockSpec(memory_space=pltpu.SMEM),
            pl.BlockSpec((3, heads, block, dim), lambda i: (0, 0, i, 0)),
            cache_block,
            cache_block,
        ],
        out_specs=[
            cache_block,
            cache_block,
            pl.BlockSpec((block, heads, dim), lambda i: (i, 0, 0)),
            pl.BlockSpec((1, heads, 128), lambda i: (i * block // per_stat, 0, 0)),
        ],
        out_shape=[
            jax.ShapeDtypeStruct(k_cache.shape, BF16),
            jax.ShapeDtypeStruct(v_cache.shape, BF16),
            jax.ShapeDtypeStruct((rows, heads, dim), F32),
            jax.ShapeDtypeStruct((rows // per_stat, heads, 128), F32),
        ],
        scratch_shapes=[pltpu.VMEM((3, heads, block, dim), F32)],
        compiler_params=pltpu.CompilerParams(dimension_semantics=("arbitrary",)),
    )(cache_len, qkv, k_cache, v_cache)


def combine_kernel(quarter, rc, cc, acc_ref, st_ref, x_hbm, w_hbm, b_ref, y_ref,
                   got_acc, got_st, fwd_acc, fwd_st, own_acc, far_acc, far_st, att,
                   w_buf, x_buf, mine, near, half, far_half, tot, from_y, from_c, from_yc, load_sem,
                   a_s, a_r, as_s, as_r, b_s, b_r, bs_s, bs_r,
                   x_s, x_r, p_s, p_r, t_s, t_r, y_s, y_r, c_s, c_r, f_s, f_r):
    heads, dim = acc_ref.shape[1:]
    n_row, n_col = quarter // rc, w_hbm.shape[1] // cc
    n = n_row * n_col
    r = lax.axis_index('sp')
    z = lax.axis_index('tp')
    core, chip_y = lax.rem(r, 2), r // 2
    mate = {'sp': chip_y * 2 + (1 - core)}
    across = {'sp': (1 - chip_y) * 2 + core}
    outer = (z == 0) | (z == 3)
    inward = {'tp': jnp.where(z == 0, 1, 2)}
    outward = {'tp': jnp.where(z == 1, 0, 3)}
    peer = {'tp': 3 - z}

    load_x = pltpu.make_async_copy(x_hbm, x_buf, load_sem.at[0])
    load_x.start()
    w_loads = []
    for j in range(n_col):
        cp = pltpu.make_async_copy(w_hbm.at[:, pl.ds(j * cc, cc)], w_buf.at[:, pl.ds(j * cc, cc)], load_sem.at[1 + j])
        cp.start()
        w_loads.append(cp)

    barrier = pltpu.get_barrier_semaphore()
    pl.semaphore_signal(barrier, inc=1, device_id=mate, device_id_type=MESH)
    pl.semaphore_signal(barrier, inc=1, device_id=across, device_id_type=MESH)

    @pl.when(outer)
    def _():
        pl.semaphore_signal(barrier, inc=1, device_id=inward, device_id_type=MESH)
        pl.semaphore_wait(barrier, 3)

    @pl.when(jnp.logical_not(outer))
    def _():
        pl.semaphore_signal(barrier, inc=1, device_id=outward, device_id_type=MESH)
        pl.semaphore_signal(barrier, inc=1, device_id=peer, device_id_type=MESH)
        pl.semaphore_wait(barrier, 4)

    def remote(src, dst, s, rcv, dev):
        return pltpu.make_async_remote_copy(src_ref=src, dst_ref=dst, send_sem=s, recv_sem=rcv, device_id=dev, device_id_type=MESH)

    mate_blocks = ((1 - chip_y) * 2 + (1 - core), chip_y * 2 + (1 - core))
    my_blocks = ((1 - chip_y) * 2 + core, chip_y * 2 + core)

    def a_stat(k):
        return remote(st_ref.at[mate_blocks[k]], got_st.at[k], as_s.at[k], as_r.at[k], mate)

    def a_copy(k, i):
        return remote(acc_ref.at[pl.ds(mate_blocks[k] * quarter + i * rc, rc)], got_acc.at[k, pl.ds(i * rc, rc)],
                      a_s.at[k, i], a_r.at[k, i], mate)

    for k in range(2):
        a_stat(k).start()
        for i in range(n_row):
            a_copy(k, i).start()

    lane = lax.broadcasted_iota(jnp.int32, (heads, 128), 1)

    def join(one, two):
        m_one, m_two = one, two
        top = jnp.maximum(m_one, m_two)
        f_one, f_two = jnp.exp(m_one - top), jnp.exp(m_two - top)
        l_one = pltpu.roll(one, 128 - quarter, 1)
        l_two = pltpu.roll(two, 128 - quarter, 1)
        total = l_one * f_one + l_two * f_two
        packed = jnp.where(lane < quarter, top, pltpu.roll(total, quarter, 1))
        return packed, f_one, f_two, total

    def b_stat():
        return remote(fwd_st, far_st, bs_s, bs_r, across)

    def b_copy(i):
        return remote(fwd_acc.at[pl.ds(i * rc, rc)], far_acc.at[pl.ds(i * rc, rc)], b_s.at[i], b_r.at[i], across)

    a_stat(0).wait()
    packed, f_one, f_two, _ = join(st_ref[my_blocks[0]], got_st[0])
    fwd_st[...] = packed
    b_stat().start()
    for i in range(n_row):
        a_copy(0, i).wait()
        mine_i = acc_ref[pl.ds(my_blocks[0] * quarter + i * rc, rc)]
        for b in range(rc):
            at = i * rc + b
            fwd_acc[at] = mine_i[b] * f_one[:, at:at + 1] + got_acc[0, at] * f_two[:, at:at + 1]
        b_copy(i).start()

    a_stat(1).wait()
    packed, f_one, f_two, _ = join(st_ref[my_blocks[1]], got_st[1])
    for i in range(n_row):
        a_copy(1, i).wait()
        mine_i = acc_ref[pl.ds(my_blocks[1] * quarter + i * rc, rc)]
        for b in range(rc):
            at = i * rc + b
            own_acc[at] = mine_i[b] * f_one[:, at:at + 1] + got_acc[1, at] * f_two[:, at:at + 1]

    b_stat().wait()
    _, g_one, g_two, total = join(packed, far_st[...])
    inv = 1.0 / jnp.where(lane < quarter, total, 1.0)
    g_one = g_one * inv
    g_two = g_two * inv

    load_x.wait()
    col_tile = lambda j: pl.ds(pl.multiple_of(j * cc, cc), cc)

    def finish(value, block, k):
        rows = pl.ds(pl.multiple_of(block * quarter + (k // n_col) * rc, rc), rc)
        cols = col_tile(lax.rem(k, n_col))
        y_ref[rows, cols] = (x_buf[rows, cols].astype(F32) + value + b_ref[:, cols].astype(F32)).astype(BF16)

    def x_copy(k):
        return remote(mine.at[k], near.at[k], x_s.at[k], x_r.at[k], inward)

    def p_copy(k):
        return remote(half.at[k], far_half.at[k], p_s.at[k], p_r.at[k], peer)

    def t_copy(k):
        return remote(tot.at[k], tot.at[k], t_s.at[k], t_r.at[k], outward)

    def y_copy(k):
        return remote(tot.at[k], from_y.at[k], y_s.at[k], y_r.at[k], across)

    def c_copy(k):
        return remote(tot.at[k], from_c.at[k], c_s.at[k], c_r.at[k], mate)

    def f_copy(k):
        return remote(from_y.at[k], from_yc.at[k], f_s.at[k], f_r.at[k], mate)

    def x_arrives(k):
        return remote(mine.at[k], near.at[k], x_s.at[k], x_r.at[k], outward)

    def t_arrives(k):
        return remote(tot.at[k], tot.at[k], t_s.at[k], t_r.at[k], inward)

    def spread(k):
        y_copy(k).start()
        c_copy(k).start()
        finish(tot[k], r, k)

    def at_lag(k, lag, do):
        if isinstance(k, int):
            if 0 <= k - lag < n:
                do(k - lag)
        else:
            pl.when((k >= lag) & (k - lag < n))(lambda: do(k - lag))

    def relay(k):
        y_copy(k).wait_recv()
        f_copy(k).start()
        finish(from_y[k], (1 - chip_y) * 2 + core, k)

    def collect(k):
        c_copy(k).wait_recv()
        finish(from_c[k], chip_y * 2 + 1 - core, k)
        f_copy(k).wait_recv()
        finish(from_yc[k], (1 - chip_y) * 2 + 1 - core, k)

    def total_inner(k):
        p_copy(k).wait_recv()
        tot[k] = half[k] + far_half[k]
        t_copy(k).start()
        spread(k)

    def total_outer(k):
        t_arrives(k).wait_recv()
        spread(k)

    def after(k):
        @pl.when(outer)
        def _():
            at_lag(k, LAGS_OUTER[0], total_outer)
            at_lag(k, LAGS_OUTER[1], relay)
            at_lag(k, LAGS_OUTER[2], collect)

        @pl.when(jnp.logical_not(outer))
        def _():
            at_lag(k, LAGS_INNER[0], total_inner)
            at_lag(k, LAGS_INNER[1], relay)
            at_lag(k, LAGS_INNER[2], collect)

    for i in range(n_row):
        b_copy(i).wait()
        for b in range(rc):
            at = i * rc + b
            own_acc[at] = own_acc[at] * g_one[:, at:at + 1] + far_acc[at] * g_two[:, at:at + 1]
        for h in range(heads):
            att[pl.ds(i * rc, rc), pl.ds(h * dim, dim)] = own_acc[pl.ds(i * rc, rc), h, :].astype(BF16)
        if i == 0:
            for cp in w_loads:
                cp.wait()

        @pl.loop(0, n_col)
        def _(j):
            k = i * n_col + j
            mine[k] = jnp.dot(att[i * rc:(i + 1) * rc], w_buf[:, col_tile(j)], preferred_element_type=F32)

            @pl.when(outer)
            def _():
                x_copy(k).start()

            @pl.when(jnp.logical_not(outer))
            def _():
                x_arrives(k).wait_recv()
                half[k] = mine[k] + near[k]
                p_copy(k).start()

            after(k)

    @pl.loop(n, n + max(LAGS_OUTER[2], LAGS_INNER[2]))
    def _(k):
        after(k)

    @pl.loop(0, n)
    def _(k):
        y_copy(k).wait_send()
        c_copy(k).wait_send()
        f_copy(k).wait_send()

        @pl.when(outer)
        def _():
            x_copy(k).wait_send()

        @pl.when(jnp.logical_not(outer))
        def _():
            p_copy(k).wait_send()
            t_copy(k).wait_send()


LAGS_INNER = (3, 6, 8)
LAGS_OUTER = (6, 9, 11)


def combine(acc, stat, tok_hidden, w_out, b_out, rc, cc):
    rows, heads, dim = acc.shape
    width = w_out.shape[1]
    quarter = rows // 4
    n_row, n_col = quarter // rc, width // cc
    n = n_row * n_col
    dma = pltpu.SemaphoreType.DMA
    part = pltpu.VMEM((quarter, heads, dim), F32)
    piece = pltpu.VMEM((n, rc, cc), F32)
    one_stat = pltpu.VMEM((heads, 128), F32)
    vmem = pl.BlockSpec(memory_space=pltpu.VMEM)
    hbm = pl.BlockSpec(memory_space=pl.ANY)
    return pl.pallas_call(
        functools.partial(combine_kernel, quarter, rc, cc),
        in_specs=[vmem, vmem, hbm, hbm, vmem],
        out_specs=vmem,
        out_shape=jax.ShapeDtypeStruct((rows, width), BF16),
        scratch_shapes=[
            pltpu.VMEM((2, quarter, heads, dim), F32), pltpu.VMEM((2, heads, 128), F32),
            part, one_stat, part, part, one_stat,
            pltpu.VMEM((quarter, heads * dim), BF16),
            pltpu.VMEM(w_out.shape, BF16), pltpu.VMEM((rows, width), BF16),
            *[piece] * 8,
            dma((1 + n_col,)),
            dma((2, n_row)), dma((2, n_row)), dma((2,)), dma((2,)),
            dma((n_row,)), dma((n_row,)), dma, dma,
            *[dma((n,))] * 12,
        ],
        compiler_params=pltpu.CompilerParams(collective_id=0, has_side_effects=True, vmem_limit_bytes=40 * 2**20),
    )(acc, stat, tok_hidden, w_out, b_out)


def solution(mesh):
    cache_spec = P('dp', 'tp', 'sp', None)
    row_spec = P('dp', None)

    def local_block(tok_hidden, cache_len, k_cache, v_cache, ln_gain, ln_bias, w_qkv, b_qkv, w_out, b_out):
        heads, dim, width = w_out.shape
        qkv = norm_project(tok_hidden, ln_gain, ln_bias, w_qkv, b_qkv)
        k_out, v_out, acc, stat = attend(qkv, cache_len, k_cache, v_cache, 16, tok_hidden.shape[0] // 4)
        y = combine(acc, stat, tok_hidden, w_out.reshape(heads * dim, width), b_out.reshape(1, width), 16, 1024)
        return y, k_out, v_out

    return jax.shard_map(
        local_block,
        mesh=mesh,
        in_specs=(row_spec, P('dp'), cache_spec, cache_spec, P(None), P(None), P(None, None, 'tp', None), P(None, 'tp', None), P('tp', None, None), P(None)),
        out_specs=(row_spec, cache_spec, cache_spec),
        check_vma=False,
    )
```

time: 287 us -> 147 us (0.51)
  waiting for transfers between devices: 192 us -> 0 us
  Pallas kernels: 0 us -> 119 us
  other arithmetic: 28.6 us -> 4.39 us
  matrix products: 31.8 us -> 16.1 us
  between operations: 14.2 us -> 0.75 us
  blocking collectives: 6.66 us -> 0 us
  local copies, waits for them, and re-layouts: 12 us -> 6.67 us
    psum x2 -> x0, waiting for transfers between devices: 192 us -> none  [the longest x1 154 us: local_block(): projected = lax.psum(partial_out, 'tp')]
    pallas_call x0 -> x2, Pallas kernels: none -> 119 us  [the longest x1 64 us: attend(): pl.pallas_call(functools.partial(attend_kernel, slots, per_stat), grid=(r...]
    dot_general x3 -> x1, matrix products: 31.8 us -> 16.1 us  [norm_project(): jnp.einsum('bm,mthd->thbd', hidden, w_qkv, preferred_element_type=F32)]
    unnamed x2 -> x0, other arithmetic: 14.2 us -> none
    pmax x1 -> x0, blocking collectives: 6.66 us -> none  [local_block(): global_max = lax.pmax(local_max, 'sp')]
    select_n x1 -> x0, other arithmetic: 4.63 us -> none  [write_token(): return jnp.where(write_mask, new_row[:, :, None, :], cache)]
    broadcast_in_dim x3 -> x0, local copies, waits for them, and re-layouts: 4.21 us -> none  [write_token(): return jnp.where(write_mask, new_row[:, :, None, :], cache)]
    convert_element_type x3 -> x1, other arithmetic: 4.12 us -> 0.01 us  [norm_project(): return (qkv_all + b_qkv.astype(F32)[:, :, None, :]).astype(BF16)]
  transfers between devices with their start and end apart: 2 -> 0, of which waited for: 2 -> 0; matrix products, arithmetic and copies ran while one was open for 0% -> 0% of each run, Pallas kernels for 0% -> 0%
where the time goes in v1:
time: 147 us; the launch traced here: 146 us
  Pallas kernels  119 us (81%)
  matrix products  16.1 us (11%)
  local copies, waits for them, and re-layouts  6.67 us (5%)
  other arithmetic  4.39 us (3%)
    pallas_call x1, Pallas kernels, attend(): pl.pallas_call(functools.partial(attend_kernel, slots, per_stat), grid=(r...  64 us
    pallas_call x1, Pallas kernels, combine(): pl.pallas_call(functools.partial(combine_kernel, quarter, rc, cc), in_spe...  54.6 us
    dot_general x1, matrix products, norm_project(): jnp.einsum('bm,mthd->thbd', hidden, w_qkv, preferred_element_type=F32)  16.1 us
    unnamed x17, local copies, waits for them, and re-layouts  6.66 us

profile of v1, /device:TPU:1, one launch (start us, length us, event | category | flops | bytes accessed | tf_op | source)
XLA Modules:
  0.0 146.5 jit_solution(9115472068852288863)
XLA Ops:
  0.6 0.0 copy-start
  0.6 0.0 copy-start.4
  0.7 0.0 copy-start.5
  0.7 0.0 copy-start.6
  0.7 0.0 copy-start.7
  0.7 2.1 %convert_reduce_fusion = f32[256]{0:T(256)S(1)} fusion(bf16[256,4096]{1,0:T(8,128)(2,1)} %x_hbm.1), kind=kLoop, calls=%fused_computation.3 | loop fusion | flops 2096896 | bytes 2098176 | tf_op jit(solution)/shard_map/reduce_sum | solution.py:18
  2.8 2.3 %fusion.4 = f32[256]{0:T(256)S(1)} fusion(bf16[256,4096]{1,0:T(8,128)(2,1)} %x_hbm.1, f32[256]{0:T(256)S(1)} %broadcast_multiply_fusion), kind=kLoop, calls=%fused_computation.6 | loop fusion | flops 4194048 | bytes 2099200 | tf_op jit(solution)/shard_map/reduce_sum | solution.py:20
  5.1 0.0 copy-done.5
  5.1 0.0 copy-done.4
  5.1 0.0 copy-done
  5.1 0.0 copy-done.6
  5.1 0.0 copy-done.7
  5.2 16.1 %fusion.18.qkv_ref = bf16[3,8,256,128]{3,2,1,0:T(8,128)(2,1)} fusion(f32[3,8,128]{2,1,0:T(8,128)S(1)} %convert_element_type.16, bf16[4096,3,8,128]{3,2,1,0:T(8,128)(2,1)} %param.16, bf16[256,4096]{1,0:T(8,128)(2,1)S(1)} %copy-done, f32[4096]{0:T(1024)S(1)} %copy-done.6, f32[4096]{0:T(1024)S(1)} %copy-done.7, f32[256]{0:T(256)S(1)} %add_rsqrt_fusion, ...), kind=kOutput, calls=%fused_computation.16 | convolution fusion | flops 6450315264 | bytes 28882944 | tf_op jit(solution)/shard_map/bm,mthd->thbd/dot_general | solution.py:22
  21.2 64.0 %shard_map.121 = (bf16[256,8,16,128]{3,2,1,0:T(8,128)(2,1)}, bf16[256,8,16,128]{3,2,1,0:T(8,128)(2,1)}, f32[256,8,128]{2,1,0:T(8,128)}, f32[4,8,128]{2,1,0:T(8,128)}) custom-call(s32[256]{0:T(256)} %len_ref.1, bf16[3,8,256,128]{3,2,1,0:T(8,128)(2,1)} %fusion.18.qkv_ref, bf16[256,8,16,128]{3,2,1,0:T(8,128)(2,1)} %k_ref.1, bf16[256,8,16,128]{3,2,1,0:T(8,128)(2,1)} %v_ref.1), custom_call_target="tpu_custom_call" | custom-call | tf_op jit(solution)/shard_map/pallas_call | solution.py:71
  85.2 0.0 copy-start.1
  85.2 3.4 %copy-done.1 = bf16[8,128,4096]{2,1,0:T(8,128)(2,1)S(1)} copy-done((bf16[8,128,4096]{2,1,0:T(8,128)(2,1)S(1)}, bf16[8,128,4096]{2,1,0:T(8,128)(2,1)}, u32[]{:S(2)}) %copy-start.1) | copy-done | bytes 8388632
  88.6 0.0 copy-start.2
  88.6 1.2 copy-done.2
  89.8 0.0 copy-start.3
  89.8 0.7 copy-done.3
  90.5 54.6 %shard_map.122 = bf16[256,4096]{1,0:T(8,128)(2,1)S(1)} custom-call(f32[256,8,128]{2,1,0:T(8,128)S(1)} %copy-done.2, f32[4,8,128]{2,1,0:T(8,128)S(1)} %copy-done.3, bf16[256,4096]{1,0:T(8,128)(2,1)S(1)} %copy-done, bf16[1024,4096]{1,0:T(8,128)(2,1)S(1)} %bitcast.12, bf16[1,4096]{1,0:T(2,128)(2,1)S(1)} %reshape.28.b_ref), custom_call_target="tpu_custom_call" | custom-call | tf_op jit(solution)/shard_map/pallas_call | solution.py:343
  145.2 1.3 copy.22
  (4 shorter events, 0.0 us)
Async XLA Ops:
  0.6 4.5 %copy-start = (bf16[256,4096]{1,0:T(8,128)(2,1)S(1)}, bf16[256,4096]{1,0:T(8,128)(2,1)}, u32[]{:S(2)}) copy-start(bf16[256,4096]{1,0:T(8,128)(2,1)} %x_hbm.1) | copy-start | bytes 6291460
  0.6 4.5 %copy-start.4 = (bf16[4096]{0:T(1024)(128)(2,1)S(1)}, bf16[4096]{0:T(1024)(128)(2,1)}, u32[]{:S(2)}) copy-start(bf16[4096]{0:T(1024)(128)(2,1)} %param.19) | copy-start | bytes 24580
  0.7 4.4 %copy-start.5 = (bf16[3,8,128]{2,1,0:T(8,128)(2,1)S(1)}, bf16[3,8,128]{2,1,0:T(8,128)(2,1)}, u32[]{:S(2)}) copy-start(bf16[3,8,128]{2,1,0:T(8,128)(2,1)} %param.17) | copy-start | bytes 18436
  0.7 4.5 %copy-start.6 = (f32[4096]{0:T(1024)S(1)}, f32[4096]{0:T(1024)}, u32[]{:S(2)}) copy-start(f32[4096]{0:T(1024)} %param.15) | copy-start | bytes 49156
  0.7 4.5 %copy-start.7 = (f32[4096]{0:T(1024)S(1)}, f32[4096]{0:T(1024)}, u32[]{:S(2)}) copy-start(f32[4096]{0:T(1024)} %param.14) | copy-start | bytes 49156
  85.2 3.4 %copy-start.1 = (bf16[8,128,4096]{2,1,0:T(8,128)(2,1)S(1)}, bf16[8,128,4096]{2,1,0:T(8,128)(2,1)}, u32[]{:S(2)}) copy-start(bf16[8,128,4096]{2,1,0:T(8,128)(2,1)} %param.18) | copy-start | bytes 25165828
  88.6 1.2 copy-start.2
  89.8 0.7 copy-start.3

commit v2 on v1

--- a/solution.py
+++ b/solution.py
@@ -8,7 +8,7 @@
 from jax.sharding import PartitionSpec as P
 
 MESH = pl.DeviceIdType.MESH
-NEG = -1e30
+NEG = float(jnp.finfo(jnp.float32).min)
 F32 = jnp.float32
 BF16 = jnp.bfloat16
 
@@ -23,7 +23,7 @@
     return (qkv_all + b_qkv.astype(F32)[:, :, None, :]).astype(BF16)
 
 
-def attend_kernel(slots, per_stat, len_ref, qkv_ref, k_ref, v_ref, ko_ref, vo_ref, acc_ref, st_ref, qkv_f32):
+def attend_kernel(slots, per_stat, len_ref, qkv_ref, k_ref, v_ref, ko_ref, vo_ref, acc_ref, st_ref, qkv_f32, scores, probs):
     rows, heads, _, dim = k_ref.shape
     step = pl.program_id(0)
     first = lax.axis_index('sp') * slots
@@ -41,27 +41,28 @@
     def _():
         st_ref[...] = jnp.zeros_like(st_ref)
 
-    stat = st_ref[0]
+    local = [len_ref[step * rows + b] - first for b in range(rows)]
     for b in range(rows):
-        local = len_ref[step * rows + b] - first
-        hit = (slot == local)[None]
+        hit = (slot == local[b])[None]
         k_new = jnp.broadcast_to(qkv_f32[1, :, b:b + 1, :], (heads, slots, dim)).astype(BF16)
         v_new = jnp.broadcast_to(qkv_f32[2, :, b:b + 1, :], (heads, slots, dim)).astype(BF16)
         k_all = jnp.where(hit, k_new, k_ref[b])
-        v_all = jnp.where(hit, v_new, v_ref[b])
         ko_ref[b] = k_all
-        vo_ref[b] = v_all
+        vo_ref[b] = jnp.where(hit, v_new, v_ref[b])
         q = qkv_f32[0, :, b, :].astype(BF16)
         s = lax.dot_general(q, k_all.reshape(flat, dim), (((1,), (1,)), ((), ())), preferred_element_type=F32)
-        valid = col_slot <= jnp.minimum(local, slots - 1)
-        s = jnp.where(valid, s * dim ** -0.5, NEG)
-        top = jnp.max(s, axis=1, keepdims=True)
-        w = jnp.where(valid, jnp.exp(s - top), 0.0)
-        total = jnp.sum(w, axis=1, keepdims=True)
-        acc_ref[b] = jnp.dot(w.astype(BF16), v_all.reshape(flat, dim), preferred_element_type=F32)
+        scores[b] = jnp.where(col_slot <= jnp.minimum(local[b], slots - 1), s * dim ** -0.5, NEG)
+    s = scores[...]
+    top = jnp.max(s, axis=2, keepdims=True)
+    w = jnp.where(s > NEG, jnp.exp(s - top), 0.0)
+    total = jnp.sum(w, axis=2, keepdims=True)
+    probs[...] = w.astype(BF16)
+    stat = st_ref[0]
+    for b in range(rows):
         at = group * rows + b
-        stat = jnp.where(lane == at, top, stat)
-        stat = jnp.where(lane == per_stat + at, total, stat)
+        stat = jnp.where(lane == at, top[b], stat)
+        stat = jnp.where(lane == per_stat + at, total[b], stat)
+        acc_ref[b] = jnp.dot(probs[b], vo_ref[b].reshape(flat, dim), preferred_element_type=F32)
     st_ref[0] = stat
 
 
@@ -89,8 +90,12 @@
             jax.ShapeDtypeStruct((rows, heads, dim), F32),
             jax.ShapeDtypeStruct((rows // per_stat, heads, 128), F32),
         ],
-        scratch_shapes=[pltpu.VMEM((3, heads, block, dim), F32)],
-        compiler_params=pltpu.CompilerParams(dimension_semantics=("arbitrary",)),
+        scratch_shapes=[
+            pltpu.VMEM((3, heads, block, dim), F32),
+            pltpu.VMEM((block, heads, heads * slots), F32),
+            pltpu.VMEM((block, heads, heads * slots), BF16),
+        ],
+        compiler_params=pltpu.CompilerParams(dimension_semantics=("arbitrary",), vmem_limit_bytes=57 * 2**20),
     )(cache_len, qkv, k_cache, v_cache)
 
 
@@ -324,8 +329,8 @@
             t_copy(k).wait_send()
 
 
-LAGS_INNER = (3, 6, 8)
-LAGS_OUTER = (6, 9, 11)
+LAGS_INNER = (4, 8, 10)
+LAGS_OUTER = (8, 12, 14)
 
 
 def combine(acc, stat, tok_hidden, w_out, b_out, rc, cc):
@@ -339,7 +344,7 @@
     piece = pltpu.VMEM((n, rc, cc), F32)
     one_stat = pltpu.VMEM((heads, 128), F32)
     vmem = pl.BlockSpec(memory_space=pltpu.VMEM)
-    hbm = pl.BlockSpec(memory_space=pl.ANY)
+    hbm = pl.BlockSpec(memory_space=pltpu.HBM)
     return pl.pallas_call(
         functools.partial(combine_kernel, quarter, rc, cc),
         in_specs=[vmem, vmem, hbm, hbm, vmem],
@@ -356,7 +361,7 @@
             dma((n_row,)), dma((n_row,)), dma, dma,
             *[dma((n,))] * 12,
         ],
-        compiler_params=pltpu.CompilerParams(collective_id=0, has_side_effects=True, vmem_limit_bytes=40 * 2**20),
+        compiler_params=pltpu.CompilerParams(collective_id=0, has_side_effects=True, vmem_limit_bytes=57 * 2**20),
     )(acc, stat, tok_hidden, w_out, b_out)
 
 
@@ -367,7 +372,7 @@
     def local_block(tok_hidden, cache_len, k_cache, v_cache, ln_gain, ln_bias, w_qkv, b_qkv, w_out, b_out):
         heads, dim, width = w_out.shape
         qkv = norm_project(tok_hidden, ln_gain, ln_bias, w_qkv, b_qkv)
-        k_out, v_out, acc, stat = attend(qkv, cache_len, k_cache, v_cache, 16, tok_hidden.shape[0] // 4)
+        k_out, v_out, acc, stat = attend(qkv, cache_len, k_cache, v_cache, 32, tok_hidden.shape[0] // 4)
         y = combine(acc, stat, tok_hidden, w_out.reshape(heads * dim, width), b_out.reshape(1, width), 16, 1024)
         return y, k_out, v_out
 

time: 147 us -> 94.1 us (0.64)
  Pallas kernels: 119 us -> 68.8 us
  local copies, waits for them, and re-layouts: 6.67 us -> 3.77 us
    pallas_call x1, Pallas kernels: 64 us -> 17.1 us  [attend(): pl.pallas_call(functools.partial(attend_kernel, slots, per_stat), grid=(r...]
    unnamed x17 -> x11, local copies, waits for them, and re-layouts: 6.66 us -> 3.15 us
    pallas_call x1, Pallas kernels: 54.6 us -> 51.8 us  [combine(): pl.pallas_call(functools.partial(combine_kernel, quarter, rc, cc), in_spe...]
where the time goes in v2:
time: 94.1 us; the launch traced here: 93.7 us
  Pallas kernels  68.8 us (73%)
  matrix products  16.1 us (17%)
  other arithmetic  4.39 us (5%)
  local copies, waits for them, and re-layouts  3.77 us (4%)
    pallas_call x1, Pallas kernels, combine(): pl.pallas_call(functools.partial(combine_kernel, quarter, rc, cc), in_spe...  51.8 us
    pallas_call x1, Pallas kernels, attend(): pl.pallas_call(functools.partial(attend_kernel, slots, per_stat), grid=(r...  17.1 us
    dot_general x1, matrix products, norm_project(): jnp.einsum('bm,mthd->thbd', hidden, w_qkv, preferred_element_type=F32)  16.1 us
    unnamed x11, local copies, waits for them, and re-layouts  3.15 us
    reduce_sum x1, other arithmetic, norm_project(): var_x = jnp.mean(centered * centered, axis=-1, keepdims=True)  2.28 us
    reduce_sum x1, other arithmetic, norm_project(): mean_x = jnp.mean(x_f32, axis=-1, keepdims=True)  2.09 us

profile of v2, /device:TPU:1, one launch (start us, length us, event | category | flops | bytes accessed | tf_op | source)
XLA Modules:
  0.0 93.7 jit_solution(13977774613576928390)
XLA Ops:
  0.6 0.0 copy-start
  0.6 0.0 copy-start.1
  0.7 0.0 copy-start.2
  0.7 0.0 copy-start.3
  0.7 0.0 copy-start.4
  0.7 2.1 %convert_reduce_fusion = f32[256]{0:T(256)S(1)} fusion(bf16[256,4096]{1,0:T(8,128)(2,1)} %x_hbm.1), kind=kLoop, calls=%fused_computation.3 | loop fusion | flops 2096896 | bytes 2098176 | tf_op jit(solution)/shard_map/reduce_sum | solution.py:18
  2.8 2.3 %fusion.4 = f32[256]{0:T(256)S(1)} fusion(bf16[256,4096]{1,0:T(8,128)(2,1)} %x_hbm.1, f32[256]{0:T(256)S(1)} %broadcast_multiply_fusion), kind=kLoop, calls=%fused_computation.6 | loop fusion | flops 4194048 | bytes 2099200 | tf_op jit(solution)/shard_map/reduce_sum | solution.py:20
  5.1 0.0 copy-done.2
  5.1 0.0 copy-done.1
  5.1 0.6 reshape.28.b_ref
  5.7 0.0 copy-done
  5.7 0.0 copy-done.3
  5.7 0.0 copy-done.4
  5.7 16.1 %fusion.18.qkv_ref = bf16[3,8,256,128]{3,2,1,0:T(8,128)(2,1)} fusion(f32[3,8,128]{2,1,0:T(8,128)S(1)} %convert_element_type.16, bf16[4096,3,8,128]{3,2,1,0:T(8,128)(2,1)} %param.16, bf16[256,4096]{1,0:T(8,128)(2,1)S(1)} %copy-done, f32[4096]{0:T(1024)S(1)} %copy-done.3, f32[4096]{0:T(1024)S(1)} %copy-done.4, f32[256]{0:T(256)S(1)} %add_rsqrt_fusion, ...), kind=kOutput, calls=%fused_computation.16 | convolution fusion | flops 6450315264 | bytes 28882944 | tf_op jit(solution)/shard_map/bm,mthd->thbd/dot_general | solution.py:22
  21.8 17.1 %shard_map.121 = (bf16[256,8,16,128]{3,2,1,0:T(8,128)(2,1)}, bf16[256,8,16,128]{3,2,1,0:T(8,128)(2,1)}, f32[256,8,128]{2,1,0:T(8,128)}, f32[4,8,128]{2,1,0:T(8,128)}) custom-call(s32[256]{0:T(256)} %len_ref.1, bf16[3,8,256,128]{3,2,1,0:T(8,128)(2,1)} %fusion.18.qkv_ref, bf16[256,8,16,128]{3,2,1,0:T(8,128)(2,1)} %k_ref.1, bf16[256,8,16,128]{3,2,1,0:T(8,128)(2,1)} %v_ref.1), custom_call_target="tpu_custom_call" | custom-call | tf_op jit(solution)/shard_map/pallas_call | solution.py:72
  38.9 51.8 %shard_map.122 = bf16[256,4096]{1,0:T(8,128)(2,1)} custom-call(f32[256,8,128]{2,1,0:T(8,128)} %get-tuple-element.7.acc_ref, f32[4,8,128]{2,1,0:T(8,128)} %get-tuple-element.8.st_ref, bf16[256,4096]{1,0:T(8,128)(2,1)} %x_hbm.1, bf16[1024,4096]{1,0:T(8,128)(2,1)} %bitcast.12, bf16[1,4096]{1,0:T(2,128)(2,1)} %reshape.28.b_ref), custom_call_target="tpu_custom_call" | custom-call | tf_op jit(solution)/shard_map/pallas_call | solution.py:348
  90.6 3.1 %copy.22 = bf16[256,4096]{1,0:T(8,128)(2,1)} copy(bf16[256,4096]{1,0:T(8,128)(2,1)} %shard_map.122) | data formatting | bytes 4194304
  (3 shorter events, 0.0 us)
Async XLA Ops:
  0.6 5.1 %copy-start = (bf16[256,4096]{1,0:T(8,128)(2,1)S(1)}, bf16[256,4096]{1,0:T(8,128)(2,1)}, u32[]{:S(2)}) copy-start(bf16[256,4096]{1,0:T(8,128)(2,1)} %x_hbm.1) | copy-start | bytes 6291460
  0.6 4.5 %copy-start.1 = (bf16[4096]{0:T(1024)(128)(2,1)S(1)}, bf16[4096]{0:T(1024)(128)(2,1)}, u32[]{:S(2)}) copy-start(bf16[4096]{0:T(1024)(128)(2,1)} %param.19) | copy-start | bytes 24580
  0.7 4.4 %copy-start.2 = (bf16[3,8,128]{2,1,0:T(8,128)(2,1)S(1)}, bf16[3,8,128]{2,1,0:T(8,128)(2,1)}, u32[]{:S(2)}) copy-start(bf16[3,8,128]{2,1,0:T(8,128)(2,1)} %param.17) | copy-start | bytes 18436
  0.7 5.1 %copy-start.3 = (f32[4096]{0:T(1024)S(1)}, f32[4096]{0:T(1024)}, u32[]{:S(2)}) copy-start(f32[4096]{0:T(1024)} %param.15) | copy-start | bytes 49156
  0.7 5.1 %copy-start.4 = (f32[4096]{0:T(1024)S(1)}, f32[4096]{0:T(1024)}, u32[]{:S(2)}) copy-start(f32[4096]{0:T(1024)} %param.14) | copy-start | bytes 49156

commit v3 on v2

--- a/solution.py
+++ b/solution.py
@@ -13,90 +13,152 @@
 BF16 = jnp.bfloat16
 
 
-def norm_project(tok_hidden, ln_gain, ln_bias, w_qkv, b_qkv):
-    x_f32 = tok_hidden.astype(F32)
-    mean_x = jnp.mean(x_f32, axis=-1, keepdims=True)
-    centered = x_f32 - mean_x
-    var_x = jnp.mean(centered * centered, axis=-1, keepdims=True)
-    hidden = (centered * lax.rsqrt(var_x + 1e-5) * ln_gain + ln_bias).astype(BF16)
-    qkv_all = jnp.einsum('bm,mthd->thbd', hidden, w_qkv, preferred_element_type=F32)
-    return (qkv_all + b_qkv.astype(F32)[:, :, None, :]).astype(BF16)
-
-
-def attend_kernel(slots, per_stat, len_ref, qkv_ref, k_ref, v_ref, ko_ref, vo_ref, acc_ref, st_ref, qkv_f32, scores, probs):
-    rows, heads, _, dim = k_ref.shape
-    step = pl.program_id(0)
+def front_kernel(slots, mc, blk, per_stat, len_ref, x_hbm, gain_ref, bias_ref, w_hbm, bqkv_ref, k_hbm, v_hbm,
+                 ko_hbm, vo_hbm, acc_ref, st_ref, x_buf, hid, w_buf, qkv, k_buf, v_buf, scores, probs,
+                 x_sem, w_sem, k_sem, v_sem, ko_sem, vo_sem):
+    rows, width = x_buf.shape
+    heads, dim = acc_ref.shape[1:]
+    ring = w_buf.shape[0]
+    n_m = width // mc
+    total = 3 * n_m
+    n_blk = rows // blk
     first = lax.axis_index('sp') * slots
-    qkv_f32[...] = qkv_ref[...].astype(F32)
-    slot = lax.broadcasted_iota(jnp.int32, (slots, dim), 0)
+
+    def w_load(t, m, slot):
+        return pltpu.make_async_copy(w_hbm.at[pl.ds(m * mc, mc), t], w_buf.at[slot], w_sem.at[slot])
+
+    def cache_copies(i):
+        part = pl.ds(i * blk, blk)
+        return (pltpu.make_async_copy(k_hbm.at[part], k_buf.at[part], k_sem.at[i]),
+                pltpu.make_async_copy(v_hbm.at[part], v_buf.at[part], v_sem.at[i]))
+
+    def out_copies(i):
+        part = pl.ds(i * blk, blk)
+        return (pltpu.make_async_copy(k_buf.at[part], ko_hbm.at[part], ko_sem.at[i]),
+                pltpu.make_async_copy(v_buf.at[part], vo_hbm.at[part], vo_sem.at[i]))
+
+    load_x = pltpu.make_async_copy(x_hbm, x_buf, x_sem)
+    load_x.start()
+    for c in range(ring):
+        w_load(c // n_m, c % n_m, c).start()
+    load_x.wait()
+
+    @pl.loop(0, rows // LN_ROWS)
+    def _(i):
+        part = pl.ds(pl.multiple_of(i * LN_ROWS, LN_ROWS), LN_ROWS)
+        x = x_buf[part].astype(F32)
+        mean = jnp.mean(x, axis=-1, keepdims=True)
+        centered = x - mean
+        var = jnp.mean(centered * centered, axis=-1, keepdims=True)
+        hid[part] = (centered * lax.rsqrt(var + 1e-5) * gain_ref[...] + bias_ref[...]).astype(BF16)
+
+    @pl.loop(0, 3)
+    def _(t):
+        bias = bqkv_ref[t].astype(F32)
+        for m in range(n_m):
+            c = t * n_m + m
+            slot = lax.rem(c, ring)
+            w_load(t, m, slot).wait()
+            w = jnp.swapaxes(w_buf[slot], 0, 1)
+            for h in range(0, heads, 2):
+                r = jnp.dot(hid[:, m * mc:(m + 1) * mc], jnp.concatenate([w[h], w[h + 1]], axis=1), preferred_element_type=F32)
+                for u in range(2):
+                    part = r[:, u * dim:(u + 1) * dim]
+                    if m:
+                        part = qkv[t, h + u] + part
+                    if m == n_m - 1:
+                        part = (part + bias[h + u:h + u + 1]).astype(BF16).astype(F32)
+                    qkv[t, h + u] = part
+            ahead = m + ring
+
+            @pl.when(c + ring < total)
+            def _():
+                w_load(t + ahead // n_m, ahead % n_m, slot).start()
+
+            for j in range(ring):
+                @pl.when(c + ring == total + j)
+                def _():
+                    for i in range(j * n_blk // ring, (j + 1) * n_blk // ring):
+                        for cp in cache_copies(i):
+                            cp.start()
+
     flat = heads * slots
+    slot_id = lax.broadcasted_iota(jnp.int32, (slots, dim), 0)
     row_id = lax.broadcasted_iota(jnp.int32, (heads, flat), 0)
     col_id = lax.broadcasted_iota(jnp.int32, (heads, flat), 1)
-    in_head = (col_id // slots) == row_id
-    col_slot = jnp.where(in_head, col_id % slots, slots)
+    col_slot = jnp.where((col_id // slots) == row_id, col_id % slots, slots)
     lane = lax.broadcasted_iota(jnp.int32, (heads, 128), 1)
-    group = lax.rem(step, per_stat // rows)
-
-    @pl.when(group == 0)
-    def _():
-        st_ref[...] = jnp.zeros_like(st_ref)
-
-    local = [len_ref[step * rows + b] - first for b in range(rows)]
-    for b in range(rows):
-        hit = (slot == local[b])[None]
-        k_new = jnp.broadcast_to(qkv_f32[1, :, b:b + 1, :], (heads, slots, dim)).astype(BF16)
-        v_new = jnp.broadcast_to(qkv_f32[2, :, b:b + 1, :], (heads, slots, dim)).astype(BF16)
-        k_all = jnp.where(hit, k_new, k_ref[b])
-        ko_ref[b] = k_all
-        vo_ref[b] = jnp.where(hit, v_new, v_ref[b])
-        q = qkv_f32[0, :, b, :].astype(BF16)
-        s = lax.dot_general(q, k_all.reshape(flat, dim), (((1,), (1,)), ((), ())), preferred_element_type=F32)
-        scores[b] = jnp.where(col_slot <= jnp.minimum(local[b], slots - 1), s * dim ** -0.5, NEG)
-    s = scores[...]
-    top = jnp.max(s, axis=2, keepdims=True)
-    w = jnp.where(s > NEG, jnp.exp(s - top), 0.0)
-    total = jnp.sum(w, axis=2, keepdims=True)
-    probs[...] = w.astype(BF16)
-    stat = st_ref[0]
-    for b in range(rows):
-        at = group * rows + b
-        stat = jnp.where(lane == at, top[b], stat)
-        stat = jnp.where(lane == per_stat + at, total[b], stat)
-        acc_ref[b] = jnp.dot(probs[b], vo_ref[b].reshape(flat, dim), preferred_element_type=F32)
-    st_ref[0] = stat
-
-
-def attend(qkv, cache_len, k_cache, v_cache, block, per_stat):
+
+    @pl.loop(0, n_blk)
+    def _(i):
+        for cp in cache_copies(i):
+            cp.wait()
+        start = i * blk
+        local = [len_ref[start + b] - first for b in range(blk)]
+        for b in range(blk):
+            at = start + b
+            hit = (slot_id == local[b])[None]
+            k_new = jnp.broadcast_to(qkv[1, :, pl.ds(at, 1), :], (heads, slots, dim)).astype(BF16)
+            v_new = jnp.broadcast_to(qkv[2, :, pl.ds(at, 1), :], (heads, slots, dim)).astype(BF16)
+            k_all = jnp.where(hit, k_new, k_buf[at])
+            k_buf[at] = k_all
+            v_buf[at] = jnp.where(hit, v_new, v_buf[at])
+            q = qkv[0, :, pl.ds(at, 1), :].reshape(heads, dim).astype(BF16)
+            s = lax.dot_general(q, k_all.reshape(flat, dim), (((1,), (1,)), ((), ())), preferred_element_type=F32)
+            scores[b] = jnp.where(col_slot <= jnp.minimum(local[b], slots - 1), s * dim ** -0.5, NEG)
+        s = scores[...]
+        top = jnp.max(s, axis=2, keepdims=True)
+        w = jnp.where(s > NEG, jnp.exp(s - top), 0.0)
+        weight = jnp.sum(w, axis=2, keepdims=True)
+        probs[...] = w.astype(BF16)
+        group = lax.rem(start, per_stat)
+        which = start // per_stat
+        stat = st_ref[which]
+        for b in range(blk):
+            at = group + b
+            stat = jnp.where(lane == at, top[b], stat)
+            stat = jnp.where(lane == per_stat + at, weight[b], stat)
+            acc_ref[start + b] = jnp.dot(probs[b], v_buf[start + b].reshape(flat, dim), preferred_element_type=F32)
+        st_ref[which] = stat
+        for cp in out_copies(i):
+            cp.start()
+
+    @pl.loop(0, n_blk)
+    def _(i):
+        for cp in out_copies(i):
+            cp.wait()
+
+
+LN_ROWS = 16
+
+
+def front(tok_hidden, cache_len, k_cache, v_cache, ln_gain, ln_bias, w_qkv, b_qkv, mc, ring, blk, per_stat):
     rows, heads, slots, dim = k_cache.shape
-    cache_block = pl.BlockSpec((block, heads, slots, dim), lambda i: (i, 0, 0, 0))
+    width = tok_hidden.shape[1]
+    vmem = pl.BlockSpec(memory_space=pltpu.VMEM)
+    hbm = pl.BlockSpec(memory_space=pltpu.HBM)
+    dma = pltpu.SemaphoreType.DMA
+    n_blk = rows // blk
     return pl.pallas_call(
-        functools.partial(attend_kernel, slots, per_stat),
-        grid=(rows // block,),
-        in_specs=[
-            pl.BlockSpec(memory_space=pltpu.SMEM),
-            pl.BlockSpec((3, heads, block, dim), lambda i: (0, 0, i, 0)),
-            cache_block,
-            cache_block,
-        ],
-        out_specs=[
-            cache_block,
-            cache_block,
-            pl.BlockSpec((block, heads, dim), lambda i: (i, 0, 0)),
-            pl.BlockSpec((1, heads, 128), lambda i: (i * block // per_stat, 0, 0)),
-        ],
+        functools.partial(front_kernel, slots, mc, blk, per_stat),
+        in_specs=[pl.BlockSpec(memory_space=pltpu.SMEM), hbm, vmem, vmem, hbm, vmem, hbm, hbm],
+        out_specs=[hbm, hbm, vmem, vmem],
         out_shape=[
             jax.ShapeDtypeStruct(k_cache.shape, BF16),
             jax.ShapeDtypeStruct(v_cache.shape, BF16),
-            jax.ShapeDtypeStruct((rows, heads, dim), F32),
-            jax.ShapeDtypeStruct((rows // per_stat, heads, 128), F32),
+            pltpu.VMEM((rows, heads, dim), F32),
+            pltpu.VMEM((rows // per_stat, heads, 128), F32),
         ],
         scratch_shapes=[
-            pltpu.VMEM((3, heads, block, dim), F32),
-            pltpu.VMEM((block, heads, heads * slots), F32),
-            pltpu.VMEM((block, heads, heads * slots), BF16),
+            pltpu.VMEM((rows, width), BF16), pltpu.VMEM((rows, width), BF16),
+            pltpu.VMEM((ring, mc, heads, dim), BF16),
+            pltpu.VMEM((3, heads, rows, dim), F32),
+            pltpu.VMEM(k_cache.shape, BF16), pltpu.VMEM(v_cache.shape, BF16),
+            pltpu.VMEM((blk, heads, heads * slots), F32), pltpu.VMEM((blk, heads, heads * slots), BF16),
+            dma, dma((ring,)), dma((n_blk,)), dma((n_blk,)), dma((n_blk,)), dma((n_blk,)),
         ],
-        compiler_params=pltpu.CompilerParams(dimension_semantics=("arbitrary",), vmem_limit_bytes=57 * 2**20),
-    )(cache_len, qkv, k_cache, v_cache)
+        compiler_params=pltpu.CompilerParams(vmem_limit_bytes=58 * 2**20),
+    )(cache_len, tok_hidden, ln_gain.reshape(1, width), ln_bias.reshape(1, width), w_qkv, b_qkv, k_cache, v_cache)
 
 
 def combine_kernel(quarter, rc, cc, acc_ref, st_ref, x_hbm, w_hbm, b_ref, y_ref,
@@ -349,7 +411,7 @@
         functools.partial(combine_kernel, quarter, rc, cc),
         in_specs=[vmem, vmem, hbm, hbm, vmem],
         out_specs=vmem,
-        out_shape=jax.ShapeDtypeStruct((rows, width), BF16),
+        out_shape=pltpu.VMEM((rows, width), BF16),
         scratch_shapes=[
             pltpu.VMEM((2, quarter, heads, dim), F32), pltpu.VMEM((2, heads, 128), F32),
             part, one_stat, part, part, one_stat,
@@ -361,7 +423,7 @@
             dma((n_row,)), dma((n_row,)), dma, dma,
             *[dma((n,))] * 12,
         ],
-        compiler_params=pltpu.CompilerParams(collective_id=0, has_side_effects=True, vmem_limit_bytes=57 * 2**20),
+        compiler_params=pltpu.CompilerParams(collective_id=0, has_side_effects=True, vmem_limit_bytes=54 * 2**20),
     )(acc, stat, tok_hidden, w_out, b_out)
 
 
@@ -371,8 +433,8 @@
 
     def local_block(tok_hidden, cache_len, k_cache, v_cache, ln_gain, ln_bias, w_qkv, b_qkv, w_out, b_out):
         heads, dim, width = w_out.shape
-        qkv = norm_project(tok_hidden, ln_gain, ln_bias, w_qkv, b_qkv)
-        k_out, v_out, acc, stat = attend(qkv, cache_len, k_cache, v_cache, 32, tok_hidden.shape[0] // 4)
+        k_out, v_out, acc, stat = front(tok_hidden, cache_len, k_cache, v_cache, ln_gain, ln_bias, w_qkv, b_qkv,
+                                        2048, 3, 32, tok_hidden.shape[0] // 4)
         y = combine(acc, stat, tok_hidden, w_out.reshape(heads * dim, width), b_out.reshape(1, width), 16, 1024)
         return y, k_out, v_out
 

time: 94.1 us -> 82.9 us (0.88)
  matrix products: 16.1 us -> 0 us
  Pallas kernels: 68.8 us -> 77.9 us
  other arithmetic: 4.39 us -> 0 us
    dot_general x1 -> x0, matrix products: 16.1 us -> none  [norm_project(): jnp.einsum('bm,mthd->thbd', hidden, w_qkv, preferred_element_type=F32)]
    pallas_call x1, Pallas kernels: 17.1 us -> 27.5 us  [front(): pl.pallas_call(functools.partial(front_kernel, slots, mc, blk, per_stat),...]
    reduce_sum x2 -> x0, other arithmetic: 4.37 us -> none  [the longest x1 2.28 us: norm_project(): var_x = jnp.mean(centered * centered, axis=-1, keepdims=True)]
    pallas_call x1, Pallas kernels: 51.8 us -> 50.4 us  [combine(): pl.pallas_call(functools.partial(combine_kernel, quarter, rc, cc), in_spe...]
    unnamed x11 -> x5, local copies, waits for them, and re-layouts: 3.15 us -> 2.89 us
where the time goes in v3:
time: 82.9 us; the launch traced here: 82.7 us
  Pallas kernels  77.9 us (94%)
  local copies, waits for them, and re-layouts  4.19 us (5%)
    pallas_call x1, Pallas kernels, combine(): pl.pallas_call(functools.partial(combine_kernel, quarter, rc, cc), in_spe...  50.4 us
    pallas_call x1, Pallas kernels, front(): pl.pallas_call(functools.partial(front_kernel, slots, mc, blk, per_stat),...  27.5 us
    unnamed x5, local copies, waits for them, and re-layouts  2.89 us

profile of v3, /device:TPU:1, one launch (start us, length us, event | category | flops | bytes accessed | tf_op | source)
XLA Modules:
  0.0 82.7 jit_solution(1216494950363719714)
XLA Ops:
  0.6 1.3 %reshape.21.b_ref = bf16[1,4096]{1,0:T(2,128)(2,1)} reshape(bf16[4096]{0:T(1024)(128)(2,1)} %param.19) | data formatting | bytes 16384 | tf_op jit(solution)/shard_map/reshape | solution.py:438
  1.9 27.5 %shard_map.121 = (bf16[256,8,16,128]{3,2,1,0:T(8,128)(2,1)}, bf16[256,8,16,128]{3,2,1,0:T(8,128)(2,1)}, f32[256,8,128]{2,1,0:T(8,128)S(1)}, f32[4,8,128]{2,1,0:T(8,128)S(1)}) custom-call(s32[256]{0:T(256)} %len_ref.1, bf16[256,4096]{1,0:T(8,128)(2,1)} %x_hbm.3, f32[1,4096]{1,0:T(1,128)} %bitcast.4, f32[1,4096]{1,0:T(1,128)} %bitcast.5, ...), custom_call_target="tpu_custom_call" | custom-call | tf_op jit(solution)/shard_map/pallas_call | solution.py:142
  29.4 0.0 copy-start
  29.4 1.0 %copy-done = f32[256,8,128]{2,1,0:T(8,128)} copy-done((f32[256,8,128]{2,1,0:T(8,128)}, f32[256,8,128]{2,1,0:T(8,128)S(1)}, u32[]{:S(2)}) %copy-start) | copy-done | bytes 1048600
  30.4 0.0 copy-start.1
  30.4 0.6 copy-done.1
  31.0 50.4 %shard_map.122 = bf16[256,4096]{1,0:T(8,128)(2,1)S(1)} custom-call(f32[256,8,128]{2,1,0:T(8,128)} %copy-done, f32[4,8,128]{2,1,0:T(8,128)} %copy-done.1, bf16[256,4096]{1,0:T(8,128)(2,1)} %x_hbm.3, bf16[1024,4096]{1,0:T(8,128)(2,1)} %bitcast.3, bf16[1,4096]{1,0:T(2,128)(2,1)} %reshape.21.b_ref), custom_call_target="tpu_custom_call" | custom-call | tf_op jit(solution)/shard_map/pallas_call | solution.py:410
  81.4 1.3 %copy.14 = bf16[256,4096]{1,0:T(8,128)(2,1)} copy(bf16[256,4096]{1,0:T(8,128)(2,1)S(1)} %shard_map.122) | data formatting | bytes 4194304
Async XLA Ops:
  29.4 1.0 %copy-start = (f32[256,8,128]{2,1,0:T(8,128)}, f32[256,8,128]{2,1,0:T(8,128)S(1)}, u32[]{:S(2)}) copy-start(f32[256,8,128]{2,1,0:T(8,128)S(1)} %get-tuple-element.7.acc_ref) | copy-start | bytes 3145732
  30.4 0.6 copy-start.1
